TPU v7x, 32 devices: a whole 2x2x4 slice. The times are simulated.
32 devices in a mesh: wide: 8 (over z, x), narrow: 4 (over y, core).
Axes of the slice: x: 2, y: 2, z: 4, core: 2. Of those that a mesh axis runs over, the one named last changes fastest.
Arguments:
- cost: float32 [1024, 16384], P('wide', 'narrow'), may hold values from 0 to 2
- plan: float32 [1024, 16384], P('wide', 'narrow'), may hold values from 0 to 2
- row_mass: float32 [1024], P('wide'), may hold values from 4096 to 28672
- col_mass: float32 [16384], P('narrow'), may hold values from 256 to 1792
- row_dual: float32 [1024], P('wide'), may hold values from -3 to 3
- col_dual: float32 [16384], P('narrow'), may hold values from -3 to 3
Outputs:
- plan_out: float32 [1024, 16384], P('wide', 'narrow')
- row_out: float32 [1024], P('wide')
- col_out: float32 [16384], P('narrow')
All inputs are finite; a program needn't handle non-finite values.
Results may differ from a plain program's by a relative error of at most 0.0001.
Values sent between devices are 32-bit elements; how exact they have to be, the bound alone decides.
A program may use at most 64 MiB of HBM per device.

v0:
```python
import math
import jax
import jax.numpy as jnp
from jax import lax
from jax.sharding import PartitionSpec as P

ITERS = 4


def shards(cost, plan, row_mass, col_mass, row_dual, col_dual):
    wide_count = lax.axis_size("wide")
    narrow_count = lax.axis_size("narrow")
    total_rows = plan.shape[0] * wide_count
    total_cols = plan.shape[1] * narrow_count
    step_base = 0.9 / math.sqrt(total_rows + total_cols)
    weight = jnp.float32(step_base)
    for step in range(ITERS):
        primal_step = step_base / weight
        dual_step = step_base * weight
        fresh = jnp.maximum(
            plan - primal_step * (cost - row_dual[:, None] - col_dual[None, :]), 0.0
        )
        change = fresh - plan
        extrap = fresh + change
        moved = jnp.sum(change * change)
        row_total = lax.psum(jnp.sum(extrap, axis=1), "narrow")
        new_row = row_dual + dual_step * (row_mass - row_total)
        row_square = jnp.sum((new_row - row_dual) ** 2)
        col_local = jnp.sum(extrap, axis=0)
        col_total = lax.psum(col_local, "wide")
        new_col = col_dual + dual_step * (col_mass - col_total)
        col_share = jnp.sum((new_col - col_dual) ** 2) / wide_count
        dual_share = row_square / narrow_count + col_share
        moved_all = lax.psum(moved, ("wide", "narrow"))
        dual_moved = lax.psum(dual_share, ("wide", "narrow"))
        weight = jnp.sqrt(weight * jnp.sqrt((dual_moved + 1.0) / (moved_all + 1.0)))
        plan, row_dual, col_dual = (fresh, new_row, new_col)
    return (plan, row_dual, col_dual)


def solution(mesh):
    in_specs = (
        P("wide", "narrow"),
        P("wide", "narrow"),
        P("wide"),
        P("narrow"),
        P("wide"),
        P("narrow"),
    )
    out_specs = (P("wide", "narrow"), P("wide"), P("narrow"))
    return jax.shard_map(shards, mesh=mesh, in_specs=in_specs, out_specs=out_specs, check_vma=False)
```

profile of v0, /device:TPU:0, one launch (start us, length us, event | category | flops | bytes accessed | tf_op | source)
XLA Modules:
  0.0 314.4 jit_solution(7714371782723744070)
XLA Ops:
  0.6 0.0 copy-start.1
  0.6 0.0 copy-start.3
  0.7 0.0 copy-start.2
  0.7 0.0 copy-start.4
  0.7 0.0 copy-start
  0.7 4.2 %multiply_reduce_fusion.2 = (f32[]{:T(128)}, f32[4096]{0:T(1024)S(1)}, f32[128]{0:T(128)S(1)}) fusion(f32[128,4096]{1,0:T(8,128)} %param.7, f32[4096]{0:T(1024)} %param.11, f32[128,4096]{1,0:T(8,128)} %param.6, f32[128]{0:T(128)} %param.10), kind=kLoop, calls=%fused_computation.6 | loop fusion | flops 5238655 | bytes 4228100 | tf_op jit(solution)/shard_map/reduce_sum | solution.py:25
  4.9 38.8 %psum.99 = f32[4096]{0:T(1024)S(1)} all-reduce(f32[4096]{0:T(1024)S(1)} %get-tuple-element.12), channel_id=1, replica_groups=mesh['wide'=8,'narrow'=4] {'wide'}, use_global_device_ids=true, to_apply=%region_4.0 | all-reduce | flops 4096 | bytes 32768 | tf_op jit(solution)/shard_map/psum | solution.py:30
  43.7 5.6 %psum.98 = f32[128]{0:T(128)S(1)} all-reduce(f32[128]{0:T(128)S(1)} %get-tuple-element.13), channel_id=1, replica_groups=mesh['wide'=8,'narrow'=4] {'narrow'}, use_global_device_ids=true, to_apply=%region_1.0 | all-reduce | flops 128 | bytes 1024 | tf_op jit(solution)/shard_map/psum | solution.py:26
  49.3 0.0 copy-done.3
  49.3 0.0 copy-done.4
  49.3 0.6 multiply_reduce_fusion.8
  50.6 0.0 copy-done.1
  50.6 0.0 copy-done.2
  50.6 0.6 multiply_reduce_fusion.5
  51.9 37.2 %all-reduce.2 = (f32[]{:T(128)}, f32[]{:T(128)}) all-reduce(f32[]{:T(128)S(6)} %add.94, f32[]{:T(128)} %get-tuple-element.11), channel_id=1, replica_groups=mesh['wide'=8,'narrow'=4] {'wide','narrow'}, use_global_device_ids=true, to_apply=%region_6.0 | all-reduce | flops 2 | bytes 16 | tf_op jit(solution)/shard_map/psum | solution.py:35
  90.5 0.0 copy-done
  90.5 3.7 %multiply_reduce_fusion.1 = (f32[]{:T(128)}, f32[128]{0:T(128)S(1)}, f32[4096]{0:T(1024)S(1)}) fusion(f32[4096]{0:T(1024)S(1)} %get-tuple-element.30, f32[128,4096]{1,0:T(8,128)} %param.6, f32[128]{0:T(128)S(1)} %get-tuple-element.32, f32[]{:T(128)S(6)} %div.39, f32[128,4096]{1,0:T(8,128)S(1)} %copy-done, f32[4096]{0:T(1024)S(1)} %copy-done.1, ...), kind=kLoop, calls=%fused_computation.4 | loop fusion | flops 7860095 | bytes 4245000 | tf_op jit(solution)/shard_map/reduce_sum | solution.py:25
  94.2 6.9 %psum.102 = f32[128]{0:T(128)S(1)} all-reduce(f32[128]{0:T(128)S(1)} %get-tuple-element.9), channel_id=1, replica_groups=mesh['wide'=8,'narrow'=4] {'narrow'}, use_global_device_ids=true, to_apply=%region_10.0 | all-reduce | flops 128 | bytes 1024 | tf_op jit(solution)/shard_map/psum | solution.py:26
  101.1 0.6 multiply_reduce_fusion.7
  102.4 35.6 %psum.103 = f32[4096]{0:T(1024)S(1)} all-reduce(f32[4096]{0:T(1024)S(1)} %get-tuple-element.10), channel_id=1, replica_groups=mesh['wide'=8,'narrow'=4] {'wide'}, use_global_device_ids=true, to_apply=%region_13.0 | all-reduce | flops 4096 | bytes 32768 | tf_op jit(solution)/shard_map/psum | solution.py:30
  138.0 0.6 multiply_reduce_fusion.4
  139.2 37.1 %all-reduce.1 = (f32[]{:T(128)}, f32[]{:T(128)}) all-reduce(f32[]{:T(128)S(6)} %add.100, f32[]{:T(128)} %get-tuple-element.8), channel_id=1, replica_groups=mesh['wide'=8,'narrow'=4] {'wide','narrow'}, use_global_device_ids=true, to_apply=%region_15.0 | all-reduce | flops 2 | bytes 16 | tf_op jit(solution)/shard_map/psum | solution.py:35
  177.8 4.2 %multiply_reduce_fusion = (f32[]{:T(128)}, f32[128]{0:T(128)S(1)}, f32[4096]{0:T(1024)S(1)}) fusion(f32[4096]{0:T(1024)S(1)} %get-tuple-element.26, f32[128,4096]{1,0:T(8,128)} %param.6, f32[128]{0:T(128)S(1)} %get-tuple-element.28, f32[]{:T(128)S(6)} %div.43, f32[4096]{0:T(1024)S(1)} %get-tuple-element.30, f32[128]{0:T(128)S(1)} %get-tuple-element.32, ...), kind=kLoop, calls=%fused_computation.2 | loop fusion | flops 10481535 | bytes 4261900 | tf_op jit(solution)/shard_map/reduce_sum | solution.py:25
  182.0 7.2 %psum.106 = f32[128]{0:T(128)S(1)} all-reduce(f32[128]{0:T(128)S(1)} %get-tuple-element.6), channel_id=1, replica_groups=mesh['wide'=8,'narrow'=4] {'narrow'}, use_global_device_ids=true, to_apply=%region_19.0 | all-reduce | flops 128 | bytes 1024 | tf_op jit(solution)/shard_map/psum | solution.py:26
  189.2 0.6 multiply_reduce_fusion.6
  190.5 35.3 %psum.107 = f32[4096]{0:T(1024)S(1)} all-reduce(f32[4096]{0:T(1024)S(1)} %get-tuple-element.7), channel_id=1, replica_groups=mesh['wide'=8,'narrow'=4] {'wide'}, use_global_device_ids=true, to_apply=%region_22.0 | all-reduce | flops 4096 | bytes 32768 | tf_op jit(solution)/shard_map/psum | solution.py:30
  225.8 0.6 multiply_reduce_fusion.3
  227.0 37.3 %all-reduce = (f32[]{:T(128)}, f32[]{:T(128)}) all-reduce(f32[]{:T(128)S(6)} %add.106, f32[]{:T(128)} %get-tuple-element.5), channel_id=1, replica_groups=mesh['wide'=8,'narrow'=4] {'wide','narrow'}, use_global_device_ids=true, to_apply=%region_24.0 | all-reduce | flops 2 | bytes 16 | tf_op jit(solution)/shard_map/psum | solution.py:35
  265.8 4.9 %fusion.6 = (f32[4096]{0:T(1024)S(1)}, f32[128]{0:T(128)S(1)}, f32[128,4096]{1,0:T(8,128)}) fusion(f32[4096]{0:T(1024)S(1)} %get-tuple-element.26, f32[128,4096]{1,0:T(8,128)} %param.6, f32[128]{0:T(128)S(1)} %get-tuple-element.28, f32[]{:T(128)S(6)} %div.43, f32[4096]{0:T(1024)S(1)} %get-tuple-element.30, f32[128]{0:T(128)S(1)} %get-tuple-element.32, ...), kind=kLoop, calls=%fused_computation.17 | loop fusion | flops 12054400 | bytes 6375948 | tf_op jit(solution)/shard_map/reduce_sum | solution.py:29
  270.7 36.8 %psum.111 = f32[4096]{0:T(1024)S(1)} all-reduce(f32[4096]{0:T(1024)S(1)} %get-tuple-element.3), channel_id=1, replica_groups=mesh['wide'=8,'narrow'=4] {'wide'}, use_global_device_ids=true, to_apply=%region_30.0 | all-reduce | flops 4096 | bytes 32768 | tf_op jit(solution)/shard_map/psum | solution.py:30
  307.5 0.6 multiply_add_fusion
  308.1 5.7 %psum.110 = f32[128]{0:T(128)S(1)} all-reduce(f32[128]{0:T(128)S(1)} %get-tuple-element.4), channel_id=1, replica_groups=mesh['wide'=8,'narrow'=4] {'narrow'}, use_global_device_ids=true, to_apply=%region_28.0 | all-reduce | flops 128 | bytes 1024 | tf_op jit(solution)/shard_map/psum | solution.py:26
  313.9 0.5 multiply_add_fusion.4
Async XLA Ops:
  0.6 49.9 %copy-start.1 = (f32[4096]{0:T(1024)S(1)}, f32[4096]{0:T(1024)}, u32[]{:S(2)}) copy-start(f32[4096]{0:T(1024)} %param.11) | copy-start | bytes 49156
  0.6 48.7 %copy-start.3 = (f32[128]{0:T(128)S(1)}, f32[128]{0:T(128)}, u32[]{:S(2)}) copy-start(f32[128]{0:T(128)} %param.10) | copy-start | bytes 1540
  0.7 49.9 %copy-start.2 = (f32[4096]{0:T(1024)S(1)}, f32[4096]{0:T(1024)}, u32[]{:S(2)}) copy-start(f32[4096]{0:T(1024)} %param.9) | copy-start | bytes 49156
  0.7 48.7 %copy-start.4 = (f32[128]{0:T(128)S(1)}, f32[128]{0:T(128)}, u32[]{:S(2)}) copy-start(f32[128]{0:T(128)} %param.8) | copy-start | bytes 1540
  0.7 89.8 %copy-start = (f32[128,4096]{1,0:T(8,128)S(1)}, f32[128,4096]{1,0:T(8,128)}, u32[]{:S(2)}) copy-start(f32[128,4096]{1,0:T(8,128)} %param.7) | copy-start | bytes 6291460
where the time goes:
time: 315 us; the launch traced here: 314 us
  blocking collectives  284 us (90%)
  other arithmetic  21.7 us (7%)
  between operations  9.03 us (3%)
    psum x4, blocking collectives, shards(): col_total = lax.psum(col_local, 'wide')  147 us
    psum x3, blocking collectives, shards(): dual_moved = lax.psum(dual_share, ('wide', 'narrow'))  112 us
    psum x4, blocking collectives, shards(): row_total = lax.psum(jnp.sum(extrap, axis=1), 'narrow')  25.5 us
    reduce_sum x3, other arithmetic, shards(): moved = jnp.sum(change * change)  12.1 us

commit v1 on v0

--- a/solution.py
+++ b/solution.py
@@ -27,7 +27,7 @@
         new_row = row_dual + dual_step * (row_mass - row_total)
         row_square = jnp.sum((new_row - row_dual) ** 2)
         col_local = jnp.sum(extrap, axis=0)
-        col_total = lax.psum(col_local, "wide")
+        col_total = jnp.sum(lax.all_gather(col_local, "wide"), axis=0)
         new_col = col_dual + dual_step * (col_mass - col_total)
         col_share = jnp.sum((new_col - col_dual) ** 2) / wide_count
         dual_share = row_square / narrow_count + col_share

time: 315 us -> 297 us (0.943)
  blocking collectives: 284 us -> 265 us
    psum x4 -> x0, blocking collectives: 147 us -> none  [shards(): col_total = lax.psum(col_local, 'wide')]
    all_gather x0 -> x4, blocking collectives: none -> 122 us  [shards(): col_total = jnp.sum(lax.all_gather(col_local, 'wide'), axis=0)]
    psum x3, blocking collectives: 112 us -> 116 us  [shards(): dual_moved = lax.psum(dual_share, ('wide', 'narrow'))]
where the time goes in v1:
time: 297 us; the launch traced here: 296 us
  blocking collectives  265 us (89%)
  other arithmetic  21.9 us (7%)
  between operations  9.07 us (3%)
    all_gather x4, blocking collectives, shards(): col_total = jnp.sum(lax.all_gather(col_local, 'wide'), axis=0)  122 us
    psum x3, blocking collectives, shards(): dual_moved = lax.psum(dual_share, ('wide', 'narrow'))  116 us
    psum x4, blocking collectives, shards(): row_total = lax.psum(jnp.sum(extrap, axis=1), 'narrow')  27.1 us
    reduce_sum x3, other arithmetic, shards(): moved = jnp.sum(change * change)  12.1 us

profile of v1, /device:TPU:0, one launch (start us, length us, event | category | flops | bytes accessed | tf_op | source)
XLA Modules:
  0.0 296.3 jit_solution(10320594225707737295)
XLA Ops:
  0.6 0.0 copy-start.1
  0.6 0.0 copy-start.3
  0.7 0.0 copy-start.2
  0.7 0.0 copy-start.4
  0.7 0.0 copy-start
  0.7 4.2 %multiply_reduce_fusion.2 = (f32[]{:T(128)}, f32[4096]{0:T(1024)S(1)}, f32[128]{0:T(128)S(1)}) fusion(f32[128,4096]{1,0:T(8,128)} %param.7, f32[4096]{0:T(1024)} %param.11, f32[128,4096]{1,0:T(8,128)} %param.6, f32[128]{0:T(128)} %param.10), kind=kLoop, calls=%fused_computation.6 | loop fusion | flops 5238655 | bytes 4228100 | tf_op jit(solution)/shard_map/reduce_sum | solution.py:25
  4.9 8.4 %psum.70 = f32[128]{0:T(128)S(1)} all-reduce(f32[128]{0:T(128)S(1)} %get-tuple-element.13), channel_id=1, replica_groups=mesh['wide'=8,'narrow'=4] {'narrow'}, use_global_device_ids=true, to_apply=%region_1.0 | all-reduce | flops 128 | bytes 1024 | tf_op jit(solution)/shard_map/psum | solution.py:26
  13.2 0.0 copy-done.3
  13.2 0.0 copy-done.4
  13.2 0.6 multiply_reduce_fusion.8
  14.5 30.9 %all-gather = f32[32768]{0:T(1024)S(1)} all-gather(f32[4096]{0:T(1024)S(1)} %get-tuple-element.12), channel_id=2, replica_groups=mesh['wide'=8,'narrow'=4] {'wide'}, dimensions={0}, use_global_device_ids=true | all-gather | bytes 147456 | tf_op jit(solution)/shard_map/all_gather | solution.py:30
  45.4 0.0 copy-done.1
  45.4 0.0 copy-done.2
  45.4 0.6 multiply_reduce_fusion.5
  46.7 38.8 %all-reduce.2 = (f32[]{:T(128)}, f32[]{:T(128)}) all-reduce(f32[]{:T(128)S(6)} %add.86, f32[]{:T(128)} %get-tuple-element.11), channel_id=1, replica_groups=mesh['wide'=8,'narrow'=4] {'wide','narrow'}, use_global_device_ids=true, to_apply=%region_6.0 | all-reduce | flops 2 | bytes 16 | tf_op jit(solution)/shard_map/psum | solution.py:35
  86.9 0.0 copy-done
  87.0 3.7 %multiply_reduce_fusion.1 = (f32[]{:T(128)}, f32[128]{0:T(128)S(1)}, f32[4096]{0:T(1024)S(1)}) fusion(f32[4096]{0:T(1024)S(1)} %get-tuple-element.30, f32[128,4096]{1,0:T(8,128)} %param.6, f32[128]{0:T(128)S(1)} %get-tuple-element.32, f32[]{:T(128)S(6)} %div.39, f32[128,4096]{1,0:T(8,128)S(1)} %copy-done, f32[4096]{0:T(1024)S(1)} %copy-done.1, ...), kind=kLoop, calls=%fused_computation.4 | loop fusion | flops 7860095 | bytes 4245000 | tf_op jit(solution)/shard_map/reduce_sum | solution.py:25
  90.7 6.8 %psum.73 = f32[128]{0:T(128)S(1)} all-reduce(f32[128]{0:T(128)S(1)} %get-tuple-element.9), channel_id=1, replica_groups=mesh['wide'=8,'narrow'=4] {'narrow'}, use_global_device_ids=true, to_apply=%region_10.0 | all-reduce | flops 128 | bytes 1024 | tf_op jit(solution)/shard_map/psum | solution.py:26
  97.5 0.6 multiply_reduce_fusion.7
  98.7 30.6 %all-gather.1 = f32[32768]{0:T(1024)S(1)} all-gather(f32[4096]{0:T(1024)S(1)} %get-tuple-element.10), channel_id=3, replica_groups=mesh['wide'=8,'narrow'=4] {'wide'}, dimensions={0}, use_global_device_ids=true | all-gather | bytes 147456 | tf_op jit(solution)/shard_map/all_gather | solution.py:30
  129.4 0.6 multiply_reduce_fusion.4
  130.6 38.1 %all-reduce.1 = (f32[]{:T(128)}, f32[]{:T(128)}) all-reduce(f32[]{:T(128)S(6)} %add.92, f32[]{:T(128)} %get-tuple-element.8), channel_id=1, replica_groups=mesh['wide'=8,'narrow'=4] {'wide','narrow'}, use_global_device_ids=true, to_apply=%region_15.0 | all-reduce | flops 2 | bytes 16 | tf_op jit(solution)/shard_map/psum | solution.py:35
  170.1 4.2 %multiply_reduce_fusion = (f32[]{:T(128)}, f32[128]{0:T(128)S(1)}, f32[4096]{0:T(1024)S(1)}) fusion(f32[4096]{0:T(1024)S(1)} %get-tuple-element.26, f32[128,4096]{1,0:T(8,128)} %param.6, f32[128]{0:T(128)S(1)} %get-tuple-element.28, f32[]{:T(128)S(6)} %div.43, f32[4096]{0:T(1024)S(1)} %get-tuple-element.30, f32[128]{0:T(128)S(1)} %get-tuple-element.32, ...), kind=kLoop, calls=%fused_computation.2 | loop fusion | flops 10481535 | bytes 4261900 | tf_op jit(solution)/shard_map/reduce_sum | solution.py:25
  174.3 6.0 %psum.76 = f32[128]{0:T(128)S(1)} all-reduce(f32[128]{0:T(128)S(1)} %get-tuple-element.6), channel_id=1, replica_groups=mesh['wide'=8,'narrow'=4] {'narrow'}, use_global_device_ids=true, to_apply=%region_19.0 | all-reduce | flops 128 | bytes 1024 | tf_op jit(solution)/shard_map/psum | solution.py:26
  180.3 0.6 multiply_reduce_fusion.6
  181.6 30.5 %all-gather.2 = f32[32768]{0:T(1024)S(1)} all-gather(f32[4096]{0:T(1024)S(1)} %get-tuple-element.7), channel_id=4, replica_groups=mesh['wide'=8,'narrow'=4] {'wide'}, dimensions={0}, use_global_device_ids=true | all-gather | bytes 147456 | tf_op jit(solution)/shard_map/all_gather | solution.py:30
  212.2 0.6 multiply_reduce_fusion.3
  213.4 38.7 %all-reduce = (f32[]{:T(128)}, f32[]{:T(128)}) all-reduce(f32[]{:T(128)S(6)} %add.98, f32[]{:T(128)} %get-tuple-element.5), channel_id=1, replica_groups=mesh['wide'=8,'narrow'=4] {'wide','narrow'}, use_global_device_ids=true, to_apply=%region_24.0 | all-reduce | flops 2 | bytes 16 | tf_op jit(solution)/shard_map/psum | solution.py:35
  253.7 4.9 %fusion.6 = (f32[4096]{0:T(1024)S(1)}, f32[128]{0:T(128)S(1)}, f32[128,4096]{1,0:T(8,128)}) fusion(f32[4096]{0:T(1024)S(1)} %get-tuple-element.26, f32[128,4096]{1,0:T(8,128)} %param.6, f32[128]{0:T(128)S(1)} %get-tuple-element.28, f32[]{:T(128)S(6)} %div.43, f32[4096]{0:T(1024)S(1)} %get-tuple-element.30, f32[128]{0:T(128)S(1)} %get-tuple-element.32, ...), kind=kLoop, calls=%fused_computation.17 | loop fusion | flops 12054400 | bytes 6375948 | tf_op jit(solution)/shard_map/reduce_sum | solution.py:29
  258.6 6.0 %psum.79 = f32[128]{0:T(128)S(1)} all-reduce(f32[128]{0:T(128)S(1)} %get-tuple-element.4), channel_id=1, replica_groups=mesh['wide'=8,'narrow'=4] {'narrow'}, use_global_device_ids=true, to_apply=%region_28.0 | all-reduce | flops 128 | bytes 1024 | tf_op jit(solution)/shard_map/psum | solution.py:26
  264.5 0.5 multiply_add_fusion.4
  265.1 30.5 %all-gather.3 = f32[32768]{0:T(1024)S(1)} all-gather(f32[4096]{0:T(1024)S(1)} %get-tuple-element.3), channel_id=5, replica_groups=mesh['wide'=8,'narrow'=4] {'wide'}, dimensions={0}, use_global_device_ids=true | all-gather | bytes 147456 | tf_op jit(solution)/shard_map/all_gather | solution.py:30
  295.6 0.6 multiply_add_fusion
  (8 shorter events, 0.3 us)
Async XLA Ops:
  0.6 44.8 %copy-start.1 = (f32[4096]{0:T(1024)S(1)}, f32[4096]{0:T(1024)}, u32[]{:S(2)}) copy-start(f32[4096]{0:T(1024)} %param.11) | copy-start | bytes 49156
  0.6 12.6 %copy-start.3 = (f32[128]{0:T(128)S(1)}, f32[128]{0:T(128)}, u32[]{:S(2)}) copy-start(f32[128]{0:T(128)} %param.10) | copy-start | bytes 1540
  0.7 44.8 %copy-start.2 = (f32[4096]{0:T(1024)S(1)}, f32[4096]{0:T(1024)}, u32[]{:S(2)}) copy-start(f32[4096]{0:T(1024)} %param.9) | copy-start | bytes 49156
  0.7 12.6 %copy-start.4 = (f32[128]{0:T(128)S(1)}, f32[128]{0:T(128)}, u32[]{:S(2)}) copy-start(f32[128]{0:T(128)} %param.8) | copy-start | bytes 1540
  0.7 86.3 %copy-start = (f32[128,4096]{1,0:T(8,128)S(1)}, f32[128,4096]{1,0:T(8,128)}, u32[]{:S(2)}) copy-start(f32[128,4096]{1,0:T(8,128)} %param.7) | copy-start | bytes 6291460
